TPU v7x, 32 devices: a whole 2x2x4 slice. The times are simulated.
32 devices in a mesh: wide: 8 (over z, x), narrow: 4 (over y, core).
Axes of the slice: x: 2, y: 2, z: 4, core: 2. Of those that a mesh axis runs over, the one named last changes fastest.
Arguments:
- tokens: bfloat16 [24, 4, 256, 768], P('wide', 'narrow'), may hold values from -6 to 6
- condition: bfloat16 [24, 768], P('wide'), may hold values from -6 to 6
- counts: int32 [8], P('wide'), may hold values from 1 to 3, as said below
- w_mod: bfloat16 [768, 4608], replicated, may hold values from -0.21875 to 0.21875
- w_qkv: bfloat16 [768, 2304], replicated, may hold values from -0.21875 to 0.21875
- w_out: bfloat16 [768, 768], replicated, may hold values from -1.75 to 1.75
- w_up: bfloat16 [768, 3072], replicated, may hold values from -0.21875 to 0.21875
- w_down: bfloat16 [3072, 768], replicated, may hold values from -0.109375 to 0.109375
- conv_attn: bfloat16 [768, 9], replicated, may hold values from -2 to 2
- conv_ffn: bfloat16 [3072, 9], replicated, may hold values from -2 to 2
- cotangent: bfloat16 [24, 4, 256, 768], P('wide', 'narrow'), may hold values from -6 to 6
Outputs:
- output: bfloat16 [24, 4, 256, 768], P('wide', 'narrow')
- token_grad: bfloat16 [24, 4, 256, 768], P('wide', 'narrow')
- cond_grad: float32 [24, 768], P('wide')
- mod_grad: float32 [768, 4608], P(('wide', 'narrow'))
- qkv_grad: float32 [768, 2304], P(('wide', 'narrow'))
- proj_grad: float32 [768, 768], P(('wide', 'narrow'))
- up_grad: float32 [768, 3072], P(('wide', 'narrow'))
- down_grad: float32 [3072, 768], P(('wide', 'narrow'))
- conv_attn_grad: float32 [768, 9], P(('wide', 'narrow'))
- conv_ffn_grad: float32 [3072, 9], P(('wide', 'narrow'))
Inputs may be any that keep to these rules, and one draw needn't show every extreme that they name: `counts`: items with index b mod 3 at or above the count of their index of wide are padding; some index of wide holds 3 live items.
All inputs are finite; a program needn't handle non-finite values.
Results may differ from a plain program's by a relative error of at most 0.017.
The roundings to bfloat16 on the way count: a program that leaves them out, or rounds other values in their place, can miss the bound.
Values may be sent and summed in bfloat16 or wider, within the bound.
A program may use at most 192 MiB of HBM per device.

v0:
```python
import math
import jax
import jax.numpy as jnp
from jax import lax
from jax.sharding import PartitionSpec as P

HEADS = 12
HEAD_DIM = 64
epsilon = 1e-06


def from_partner(shard, axis, bit):
    return lax.ppermute(shard, axis, [(i, i ^ 1 << bit) for i in range(lax.axis_size(axis))])


def normed(field_map):
    average = jnp.mean(field_map, -1, keepdims=True)
    centred = field_map - average
    variance = jnp.mean(centred * centred, -1, keepdims=True)
    return centred * lax.rsqrt(variance + epsilon)


def modulate(field_map, shift, scale):
    return normed(field_map) * (1.0 + scale) + shift


def gelu_tanh(field_map):
    return jax.nn.gelu(field_map, approximate=True)


def attn_across(outgoing):
    return from_partner(outgoing, "narrow", 0)


def attn_down(outgoing):
    return from_partner(outgoing, "narrow", 1)


def ffn_across(outgoing):
    return from_partner(outgoing, "narrow", 0)


def ffn_down(outgoing):
    return from_partner(outgoing, "narrow", 1)


def extend(field_map, row_half, col_half, across, down):
    outgoing = jnp.where(col_half == 0, field_map[:, :, -1:], field_map[:, :, :1])
    incoming = across(outgoing)
    zeros_rim = jnp.zeros_like(incoming)
    left_rim = jnp.where(col_half == 1, incoming, zeros_rim)
    right_rim = jnp.where(col_half == 0, incoming, zeros_rim)
    widened = jnp.concatenate([left_rim, field_map, right_rim], 2)
    outgoing = jnp.where(row_half == 0, widened[:, -1:], widened[:, :1])
    incoming = down(outgoing)
    zeros_rim = jnp.zeros_like(incoming)
    top_rim = jnp.where(row_half == 1, incoming, zeros_rim)
    bottom_rim = jnp.where(row_half == 0, incoming, zeros_rim)
    return jnp.concatenate([top_rim, widened, bottom_rim], 1)


def apply_taps(padded, kernel, side_len, flipped):
    summed = jnp.zeros((padded.shape[0], side_len, side_len, padded.shape[3]), jnp.float32)
    weights_f = kernel.astype(jnp.float32)
    for stencil in range(9):
        row_off = stencil // 3
        col_off = stencil % 3
        if flipped:
            row_off = 2 - row_off
            col_off = 2 - col_off
        window = padded[:, row_off : row_off + side_len, col_off : col_off + side_len].astype(
            jnp.float32
        )
        summed = summed + window * weights_f[:, stencil]
    return summed


def tap_grads(padded, grad_map, side_len):
    grad_f = grad_map.astype(jnp.float32)
    columns = []
    for stencil in range(9):
        row_off = stencil // 3
        col_off = stencil % 3
        window = padded[:, row_off : row_off + side_len, col_off : col_off + side_len].astype(
            jnp.float32
        )
        columns.append(jnp.sum(window * grad_f, axis=(0, 1, 2)))
    return jnp.stack(columns, 1)


def to_groups(field_map):
    count, side_len, _, channels = field_map.shape
    quarter = side_len // 2
    pieces = field_map.reshape(count, quarter, 2, quarter, 2, channels).transpose(0, 2, 4, 1, 3, 5)
    pieces = pieces.reshape(count, 4, quarter * quarter, channels)
    incoming = lax.all_to_all(pieces, "narrow", split_axis=1, concat_axis=1, tiled=True)
    return incoming.reshape(count, 4 * quarter * quarter, channels)


def to_quads(group_rows):
    count, rows_all, channels = group_rows.shape
    pieces = group_rows.reshape(count, 4, rows_all // 4, channels)
    incoming = lax.all_to_all(pieces, "narrow", split_axis=1, concat_axis=1, tiled=True)
    quarter = math.isqrt(rows_all // 4)
    incoming = incoming.reshape(count, 2, 2, quarter, quarter, channels).transpose(0, 3, 1, 4, 2, 5)
    return incoming.reshape(count, 2 * quarter, 2 * quarter, channels)


def split_heads(groups, w_qkv):
    count, rows_all, _ = groups.shape
    triple = jnp.dot(groups, w_qkv, preferred_element_type=jnp.float32).astype(jnp.bfloat16)
    triple = triple.reshape(count, rows_all, 3, HEADS, HEAD_DIM)
    return (triple[:, :, 0], triple[:, :, 1], triple[:, :, 2])


def score(queries, key_rows):
    return jnp.einsum(
        "iqhe,ikhe->ihqk", queries, key_rows, preferred_element_type=jnp.float32
    ) * HEAD_DIM ** (-0.5)


def narrow_sum(part):
    for bit in range(lax.axis_size("narrow").bit_length() - 1):
        part = part + from_partner(part, "narrow", bit)
    return part


def wide_gather(block):
    count = lax.axis_size("wide")
    place = lax.axis_index("wide")
    held = block[None]
    for bit in range(count.bit_length() - 1):
        other = from_partner(held, "wide", bit)
        mine_high = place >> bit & 1
        low = jnp.where(mine_high == 1, other, held)
        high = jnp.where(mine_high == 1, held, other)
        held = jnp.concatenate([low, high], 0)
    return held.reshape((count * block.shape[0],) + block.shape[1:])


def split_dot(exact, coarse, dims):
    high = exact.astype(jnp.bfloat16)
    low = (exact - high.astype(jnp.float32)).astype(jnp.bfloat16)
    high_dot = lax.dot_general(high, coarse, (dims, ((), ())), preferred_element_type=jnp.float32)
    low_dot = lax.dot_general(low, coarse, (dims, ((), ())), preferred_element_type=jnp.float32)
    return high_dot + low_dot


def halving_sum(blocks, colour):
    wide_bits = lax.axis_size("wide").bit_length() - 1
    narrow_bits = lax.axis_size("narrow").bit_length() - 1
    order = [("narrow", 0)]
    first = [("wide", 0), ("narrow", 1)]
    order += first if colour == 0 else first[::-1]
    order += [("wide", bit) for bit in range(1, wide_bits)]
    names = [("wide", bit) for bit in range(wide_bits - 1, -1, -1)]
    names += [("narrow", bit) for bit in range(narrow_bits - 1, -1, -1)]
    held = blocks.reshape((2,) * len(names) + blocks.shape[1:])
    for step, (axis, bit) in enumerate(order):
        where = names.index((axis, bit))
        names.pop(where)
        mine = lax.axis_index(axis) >> bit & 1
        keep = lax.dynamic_index_in_dim(held, mine, where, keepdims=False)
        give = lax.dynamic_index_in_dim(held, 1 - mine, where, keepdims=False)
        got = from_partner(give, axis, bit)
        held = keep.astype(jnp.float32) + got.astype(jnp.float32)
        if step < len(order) - 1:
            held = held.astype(jnp.bfloat16)
    return held


def shards(
    tokens, condition, counts, w_mod, w_qkv, w_out, w_up, w_down, conv_attn, conv_ffn, cotangent
):
    item_count, _, quad_rows, channels = tokens.shape
    half_side = math.isqrt(quad_rows)
    corner = lax.axis_index("narrow")
    row_half = corner // 2
    col_half = corner % 2
    living = (jnp.arange(item_count, dtype=jnp.int32) < counts[0]).astype(jnp.float32)[
        :, None, None, None
    ]
    start_map = tokens.reshape(item_count, half_side, half_side, channels).astype(jnp.float32)
    cond_f = condition.astype(jnp.float32)
    lifted = jax.nn.silu(cond_f).astype(jnp.bfloat16)
    all_lifted = wide_gather(lifted)
    modulation = jnp.dot(lifted, w_mod, preferred_element_type=jnp.float32).reshape(
        item_count, 6, channels
    )
    pieces = [modulation[:, place][:, None, None, :] for place in range(6)]
    shift_a, scale_a, gate_a, shift_f, scale_f, gate_f = pieces
    first_f, pull_attn_norm = jax.vjp(modulate, start_map, shift_a, scale_a)
    first_in = first_f.astype(jnp.bfloat16)
    padded_attn = extend(first_in, row_half, col_half, attn_across, attn_down)
    mixed_map = apply_taps(padded_attn, conv_attn, half_side, False).astype(jnp.bfloat16)
    groups = to_groups(mixed_map)
    queries, key_rows, values = split_heads(groups, w_qkv)
    scores = score(queries, key_rows)
    peak = jnp.max(scores, -1, keepdims=True)
    raised_exp = jnp.exp(scores - peak)
    summed = jnp.sum(raised_exp, -1, keepdims=True)
    attn_probs = (raised_exp / summed).astype(jnp.bfloat16)
    log_total = peak + jnp.log(summed)
    attended = jnp.einsum("ihqk,ikhe->iqhe", attn_probs, values, preferred_element_type=jnp.float32)
    attended = attended.astype(jnp.bfloat16).reshape(item_count, quad_rows, channels)
    returned = to_quads(attended)
    branch = jnp.dot(returned, w_out, preferred_element_type=jnp.float32)
    hidden_one = start_map + gate_a * branch
    second_f, pull_ffn_norm = jax.vjp(modulate, hidden_one, shift_f, scale_f)
    second = second_f.astype(jnp.bfloat16)
    raised = jnp.dot(second, w_up, preferred_element_type=jnp.float32).astype(jnp.bfloat16)
    padded_ffn = extend(raised, row_half, col_half, ffn_across, ffn_down)
    filtered = apply_taps(padded_ffn, conv_ffn, half_side, False)
    activated = gelu_tanh(filtered).astype(jnp.bfloat16)
    branch_two = jnp.dot(activated, w_down, preferred_element_type=jnp.float32)
    output = ((hidden_one + gate_f * branch_two) * living).astype(jnp.bfloat16)
    grad_res = (
        cotangent.reshape(item_count, half_side, half_side, channels).astype(jnp.float32) * living
    )
    d_gate_f = jnp.sum(grad_res * branch_two, (1, 2))
    d_branch_two = (grad_res * gate_f).astype(jnp.bfloat16)
    down_grad = jnp.einsum(
        "ixyf,ixyd->fd", activated, d_branch_two, preferred_element_type=jnp.float32
    )
    d_activated = jnp.einsum(
        "ixyd,fd->ixyf", d_branch_two, w_down, preferred_element_type=jnp.float32
    )
    again = jnp.dot(second, w_up, preferred_element_type=jnp.float32).astype(jnp.bfloat16)
    kept_pad = extend(again, row_half, col_half, ffn_across, ffn_down)
    kept_filter = apply_taps(kept_pad, conv_ffn, half_side, False)
    _, gelu_pull = jax.vjp(gelu_tanh, kept_filter)
    d_filtered = gelu_pull(d_activated)[0].astype(jnp.bfloat16)
    conv_ffn_grad = tap_grads(kept_pad, d_filtered, half_side)
    d_padded_ffn = extend(d_filtered, row_half, col_half, ffn_across, ffn_down)
    d_raised = apply_taps(d_padded_ffn, conv_ffn, half_side, True).astype(jnp.bfloat16)
    up_grad = jnp.einsum("ixyd,ixyf->df", second, d_raised, preferred_element_type=jnp.float32)
    d_second = jnp.einsum("ixyf,df->ixyd", d_raised, w_up, preferred_element_type=jnp.float32)
    d_hidden_part, d_shift_f, d_scale_f = pull_ffn_norm(d_second)
    d_hidden = grad_res + d_hidden_part
    d_gate_a = jnp.sum(d_hidden * branch, (1, 2))
    d_branch = (d_hidden * gate_a).astype(jnp.bfloat16)
    proj_grad = jnp.einsum("ixyd,ixye->de", returned, d_branch, preferred_element_type=jnp.float32)
    d_returned = jnp.einsum(
        "ixye,de->ixyd", d_branch, w_out, preferred_element_type=jnp.float32
    ).astype(jnp.bfloat16)
    d_attended = to_groups(d_returned).reshape(item_count, quad_rows, HEADS, HEAD_DIM)
    queries, key_rows, values = split_heads(groups, w_qkv)
    scores = score(queries, key_rows)
    exact = jnp.exp(scores - log_total)
    rounded = exact.astype(jnp.bfloat16)
    d_probs = jnp.einsum("iqhe,ikhe->ihqk", d_attended, values, preferred_element_type=jnp.float32)
    d_values = jnp.einsum(
        "ihqk,iqhe->ikhe", rounded, d_attended, preferred_element_type=jnp.float32
    )
    d_scores = (exact * (d_probs - jnp.sum(d_probs * exact, -1, keepdims=True))).astype(
        jnp.bfloat16
    )
    d_queries = jnp.einsum(
        "ihqk,ikhe->iqhe", d_scores, key_rows, preferred_element_type=jnp.float32
    ) * HEAD_DIM ** (-0.5)
    d_keys = jnp.einsum(
        "ihqk,iqhe->ikhe", d_scores, queries, preferred_element_type=jnp.float32
    ) * HEAD_DIM ** (-0.5)
    d_triple = (
        jnp.stack([d_queries, d_keys, d_values], 2)
        .astype(jnp.bfloat16)
        .reshape(item_count, quad_rows, 3 * channels)
    )
    qkv_grad = jnp.einsum("iqd,iqe->de", groups, d_triple, preferred_element_type=jnp.float32)
    d_groups = jnp.einsum(
        "iqe,de->iqd", d_triple, w_qkv, preferred_element_type=jnp.float32
    ).astype(jnp.bfloat16)
    d_mixed = to_quads(d_groups)
    conv_attn_grad = tap_grads(padded_attn, d_mixed, half_side)
    d_padded_attn = extend(d_mixed, row_half, col_half, attn_across, attn_down)
    d_first = apply_taps(d_padded_attn, conv_attn, half_side, True).astype(jnp.bfloat16)
    d_start, d_shift_a, d_scale_a = pull_attn_norm(d_first.astype(jnp.float32))
    token_grad = (d_hidden + d_start).astype(jnp.bfloat16).reshape(tokens.shape)
    flat_parts = [
        d_shift_a.reshape(item_count, channels),
        d_scale_a.reshape(item_count, channels),
        d_gate_a,
        d_shift_f.reshape(item_count, channels),
        d_scale_f.reshape(item_count, channels),
        d_gate_f,
    ]
    d_modulation = jnp.stack(flat_parts, 1).reshape(item_count, 6 * channels)
    d_modulation = narrow_sum(d_modulation)
    _, silu_pull = jax.vjp(jax.nn.silu, cond_f)
    d_lifted = split_dot(d_modulation, w_mod, ((1,), (1,)))
    cond_grad = silu_pull(d_lifted)[0]
    all_modulation = wide_gather(d_modulation)
    block_rows = channels // (lax.axis_size("wide") * lax.axis_size("narrow"))
    own_block = lax.axis_index("wide") * lax.axis_size("narrow") + corner
    own_lifted = lax.dynamic_slice_in_dim(all_lifted, own_block * block_rows, block_rows, 1)
    mod_sum = split_dot(all_modulation, own_lifted, ((0,), (0,))).T
    blocks = lax.axis_size("wide") * lax.axis_size("narrow")
    up_blocks = up_grad.astype(jnp.bfloat16).reshape(blocks, -1, up_grad.shape[1])
    down_blocks = down_grad.astype(jnp.bfloat16).reshape(blocks, -1, channels)
    up_sum = halving_sum(up_blocks, 0)
    down_sum = halving_sum(down_blocks, 1)
    qkv_blocks = qkv_grad.astype(jnp.bfloat16).reshape(blocks, -1, 3 * channels)
    proj_blocks = proj_grad.astype(jnp.bfloat16).reshape(blocks, -1, channels)
    taps = jnp.concatenate(
        [conv_attn_grad.reshape(blocks, -1), conv_ffn_grad.reshape(blocks, -1)], 1
    )
    rows = qkv_blocks.shape[1]
    taps_len = taps.shape[1]
    taps_wide = -(-taps_len // (rows * 128)) * 128
    taps = jnp.pad(taps, ((0, 0), (0, rows * taps_wide - taps_len)))
    taps = taps.astype(jnp.bfloat16).reshape(blocks, rows, taps_wide)
    left_sum = halving_sum(qkv_blocks[:, :, : 2 * channels], 0)
    right = jnp.concatenate([qkv_blocks[:, :, 2 * channels :], proj_blocks, taps], 2)
    right_sum = halving_sum(right, 1)
    qkv_sum = jnp.concatenate([left_sum, right_sum[:, :channels]], 1)
    proj_sum = right_sum[:, channels : 2 * channels]
    tap_sums = right_sum[:, 2 * channels :].reshape(-1)
    attn_len = conv_attn_grad.size // blocks
    conv_attn_sum = tap_sums[:attn_len].reshape(-1, 9)
    conv_ffn_sum = tap_sums[attn_len:taps_len].reshape(-1, 9)
    return (
        output.reshape(tokens.shape),
        token_grad,
        cond_grad,
        mod_sum,
        qkv_sum,
        proj_sum,
        up_sum,
        down_sum,
        conv_attn_sum,
        conv_ffn_sum,
    )


def solution(mesh):
    in_specs = (
        P("wide", "narrow", None, None),
        P("wide", None),
        P("wide"),
        P(),
        P(),
        P(),
        P(),
        P(),
        P(),
        P(),
        P("wide", "narrow", None, None),
    )
    out_specs = (
        P("wide", "narrow", None, None),
        P("wide", "narrow", None, None),
        P("wide", None),
        P(("wide", "narrow"), None),
        P(("wide", "narrow"), None),
        P(("wide", "narrow"), None),
        P(("wide", "narrow"), None),
        P(("wide", "narrow"), None),
        P(("wide", "narrow"), None),
        P(("wide", "narrow"), None),
    )
    return jax.shard_map(shards, mesh=mesh, in_specs=in_specs, out_specs=out_specs, check_vma=False)
```

profile of v0, /device:TPU:0, one launch (start us, length us, event | category | flops | bytes accessed | tf_op | source)
XLA Modules:
  0.0 598.8 jit_solution(1541009015088107314)
XLA Ops:
  5.1 4.7 fusion.146
  47.6 4.6 all-to-all-start
  55.2 12.9 %all-to-all-done = bf16[3,4,64,768]{3,2,0,1:T(8,128)(2,1)} async-done(((bf16[3,4,64,768]{3,2,0,1:T(8,128)(2,1)}), bf16[3,4,64,768]{3,2,0,1:T(8,128)(2,1)}, u32[]{:S(2)}, u32[]{:S(2)}) %all-to-all-start) | async-done | bytes 1179680 | tf_op jit(solution)/shard_map/all_to_all | solution.py:96
  74.8 5.8 copy.105
  87.9 4.6 fusion.94
  92.5 4.6 reshape_reshape.12
  97.1 5.1 copy.110
  102.2 4.8 all-to-all-start.1
  114.7 8.1 %all-to-all-done.1 = bf16[3,4,64,768]{3,2,0,1:T(8,128)(2,1)} async-done(((bf16[3,4,64,768]{3,2,0,1:T(8,128)(2,1)}), bf16[3,4,64,768]{3,2,0,1:T(8,128)(2,1)}, u32[]{:S(2)}, u32[]{:S(2)}) %all-to-all-start.1) | async-done | bytes 1179680 | tf_op jit(solution)/shard_map/all_to_all | solution.py:103
  130.1 5.0 fusion.142
  149.9 10.7 %collective-permute-done.3 = bf16[3,1,18,3072]{3,2,1,0:T(8,128)(2,1)} collective-permute-done((bf16[3,1,18,3072]{3,2,1,0:T(8,128)(2,1)}, bf16[3,1,18,3072]{3,2,1,0:T(8,128)(2,1)}, u32[]{:S(2)}, u32[]{:S(2)}) %collective-permute-start.3) | collective-permute-done | bytes 331808 | tf_op jit(solution)/shard_map/ppermute | solution.py:13
  161.8 12.1 %maximum_maximum_fusion = (bf16[3,17,18,3072]{3,2,1,0:T(8,128)(2,1)S(1)}, bf16[3,17,18,3072]{3,2,1,0:T(8,128)(2,1)S(1)}) fusion(bf16[3,16,1,3072]{3,2,1,0:T(2,128)(2,1)} %copy-done.27, bf16[3,16,16,3072]{3,2,1,0:T(8,128)(2,1)} %copy-done.5, bf16[3,16,1,3072]{3,2,1,0:T(2,128)(2,1)} %copy-done.25, bf16[3,1,18,3072]{3,2,1,0:T(8,128)(2,1)S(1)} %get-tuple-element.121, ...), kind=kLoop, calls=%fused_computation.61 | loop fusion | flops 45121536 | bytes 17252352 | tf_op jit(solution)/shard_map/concatenate | solution.py:59
  174.1 15.6 %fusion.7 = f32[3,16,16,3072]{3,2,1,0:T(8,128)} fusion(bf16[3,16,16,3072]{3,2,1,0:T(8,128)(2,1)S(1)} %bitcast.307, bf16[3,16,1,3072]{3,2,1,0:T(2,128)(2,1)} %copy-done.27, bf16[3,16,1,3072]{3,2,1,0:T(2,128)(2,1)S(1)} %copy-done.26, f32[3072]{0:T(1024)S(1)} %bitcast.354, f32[3072]{0:T(1024)S(1)} %bitcast.352, f32[3072]{0:T(1024)S(1)} %bitcast.350, ...), kind=kLoop, calls=%fused_computation.28 | loop fusion | flops 75497472 | bytes 43167744 | tf_op jit(solution)/shard_map/add | solution.py:74
  189.7 35.1 %fusion.29 = (bf16[3072]{0:T(1024)(128)(2,1)}, bf16[3072]{0:T(1024)(128)(2,1)}, bf16[3072]{0:T(1024)(128)(2,1)}, bf16[3072]{0:T(1024)(128)(2,1)}, bf16[3072]{0:T...) fusion(bf16[3,17,18,3072]{3,2,1,0:T(8,128)(2,1)} %copy-done.4, ...), kind=kOutput, calls=%fused_computation.50 | convolution fusion | flops 3753612288 | bytes 53738508 | tf_op jit(solution)/shard_map/ixyd,fd->ixyf/dot_general | solution.py:225
  237.7 9.7 %bitcast_convert_fusion = bf16[3072,768]{1,0:T(8,128)(2,1)} fusion(bf16[3,16,16,768]{3,2,1,0:T(8,128)(2,1)S(1)} %bitcast.359, f32[3]{0:T(128)S(1)} %compare_convert_fusion, f32[3,768]{1,0:T(4,128)S(1)} %copy-done.112, f32[3,16,16,3072]{3,2,1,0:T(8,128)} %fusion.7), kind=kOutput, calls=%fused_computation.51 | convolution fusion | flops 3649830912 | bytes 15344652 | tf_op jit(solution)/shard_map/ixyf,ixyd->fd/dot_general | solution.py:222
  267.8 10.0 %pad_maximum_fusion.1 = (bf16[3,17,18,3072]{3,2,1,0:T(8,128)(2,1)S(1)}, bf16[3,17,18,3072]{3,2,1,0:T(8,128)(2,1)S(1)}) fusion(bf16[3,1,18,3072]{3,2,1,0:T(8,128)(2,1)S(1)} %get-tuple-element.119, bf16[3,16,1,3072]{3,2,1,0:T(2,128)(2,1)S(1)} %copy-done.31, bf16[3,16,16,3072]{3,2,1,0:T(8,128)(2,1)S(1)} %bitcast.305, ...), kind=kLoop, calls=%fused_computation.63 | loop fusion | flops 45121536 | bytes 17252352 | tf_op jit(solution)/shard_map/concatenate | solution.py:59
  278.0 15.8 %fusion.20 = bf16[3,16,16,3072]{3,2,1,0:T(8,128)(2,1)} fusion(bf16[3,16,16,3072]{3,2,1,0:T(8,128)(2,1)S(1)} %bitcast.305, bf16[3,17,18,3072]{3,2,1,0:T(8,128)(2,1)S(1)} %get-tuple-element.100, bf16[3,16,1,3072]{3,2,1,0:T(2,128)(2,1)S(1)} %copy-done.29, bf16[3,16,1,3072]{3,2,1,0:T(2,128)(2,1)} %copy-done.30, ...), kind=kLoop, calls=%fused_computation.41 | loop fusion | flops 77856768 | bytes 38449152 | tf_op jit(solution)/shard_map/convert_element_type | solution.py:235
  293.9 8.6 %multiply_reduce_fusion.5 = (f32[3,16,16]{2,1,0:T(8,128)S(1)}, f32[3,16,16,768]{3,2,1,0:T(8,128)S(1)}) fusion(f32[3,16,16,768]{3,2,1,0:T(8,128)} %copy-done.12, f32[3,768]{1,0:T(4,128)S(1)} %copy-done.93, f32[3,16,16]{2,1,0:T(8,128)S(1)} %copy-done.53, bf16[3,16,16,3072]{3,2,1,0:T(8,128)(2,1)} %fusion.20, bf16[768,3072]{1,0:T(8,128)(2,1)} %param.17), kind=kOutput, calls=%fused_computation.170 | convolution fusion | flops 3626237184 | bytes 14171136 | tf_op jit(solution)/shard_map/ixyf,df->ixyd/dot_general | solution.py:237
  302.6 6.4 %bitcast_convert_fusion.1 = bf16[768,3072]{1,0:T(8,128)(2,1)} fusion(bf16[3,16,16,3072]{3,2,1,0:T(8,128)(2,1)S(1)} %copy-done.33, f32[3,16,16,768]{3,2,1,0:T(8,128)S(1)} %copy-done.13, f32[3,768]{1,0:T(4,128)S(1)} %copy-done.115, f32[3,768]{1,0:T(4,128)S(1)} %copy-done.93, f32[3,16,16]{2,1,0:T(8,128)S(1)} %copy-done.81, f32[3,16,16]{2,1,0:T(8,128)S(1)} %copy-done.53), kind=kOutput, calls=%fused_computation.52 | convolution fusion | flops 3629187072 | bytes 11821056 | tf_op jit(solution)/shard_map/ixyd,ixyf->df/dot_general | solution.py:236
  311.5 10.4 %fusion.86 = (f32[3,768]{1,0:T(4,128)}, bf16[3,16,16,768]{3,2,1,0:T(8,128)(2,1)}, f32[3,768]{1,0:T(4,128)}, f32[3,16,16,768]{3,2,1,0:T(8,128)S(1)}) fusion(bf16[3,16,16,768]{3,2,1,0:T(8,128)(2,1)S(1)} %bitcast.360, f32[3]{0:T(128)S(1)} %compare_convert_fusion, f32[3,16,16,768]{3,2,1,0:T(8,128)S(1)} %copy-done.13, f32[3,768]{1,0:T(4,128)S(1)} %copy-done.113, ...), kind=kOutput, calls=%fused_computation.159 | convolution fusion | flops 3655724544 | bytes 26001420 | tf_op jit(solution)/shard_map/dot_general | solution.py:215
  352.0 5.2 copy.121
  361.7 6.8 %fusion.87 = bf16[3,256,1,12,64]{1,4,3,0,2:T(8,128)(2,1)} fusion(bf16[3,256,12,64]{1,3,2,0:T(8,128)(2,1)} %reshape_reshape.13, f32[3,12,256,256]{2,3,1,0:T(8,128)} %copy-done.1, f32[3,12,256]{2,1,0:T(8,128)} %log_add_fusion), kind=kOutput, calls=%fused_computation.182 | convolution fusion | flops 309067776 | bytes 11833344 | tf_op jit(solution)/shard_map/ihqk,iqhe->ikhe/dot_general | solution.py:252
  368.5 8.2 %multiply_reduce_fusion = (f32[3,12,256]{2,1,0:T(8,128)}, f32[3,12,256,256]{2,3,1,0:T(8,128)}) fusion(f32[3,12,256,256]{2,3,1,0:T(8,128)} %copy-done.1, f32[3,12,256]{2,1,0:T(8,128)S(1)} %copy-done.46, bf16[3,256,12,64]{1,3,2,0:T(8,128)(2,1)S(1)} %copy-done.15, bf16[3,256,3,12,64]{1,4,3,2,0:T(8,128)(2,1)} %bitcast.310), kind=kOutput, calls=%fused_computation.54 | convolution fusion | flops 311417856 | bytes 21307392 | tf_op jit(solution)/shard_map/iqhe,ikhe->ihqk/dot_general | solution.py:251
  376.8 11.3 %multiply_convert_fusion = bf16[3,12,256,256]{2,3,1,0:T(8,128)(2,1)} fusion(f32[3,12,256,256]{2,3,1,0:T(8,128)} %get-tuple-element.170, f32[3,12,256,256]{2,3,1,0:T(8,128)} %copy-done.1, f32[3,12,256]{2,1,0:T(8,128)} %get-tuple-element.169, f32[3,12,256]{2,1,0:T(8,128)} %log_add_fusion), kind=kLoop, calls=%fused_computation.53 | loop fusion | flops 11796480 | bytes 23666688 | tf_op jit(solution)/shard_map/convert_element_type | solution.py:255
  404.3 5.3 bitcast_convert_fusion.2
  430.0 7.7 %fusion.78 = (bf16[768]{0:T(1024)(128)(2,1)}, bf16[768]{0:T(1024)(128)(2,1)}, bf16[768]{0:T(1024)(128)(2,1)}, bf16[768]{0:T(1024)(128)(2,1)S(1)}, bf16[768]{0:T(...) fusion(bf16[3,16,16,768]{3,2,1,0:T(8,128)(2,1)} %reshape.319, ...), kind=kLoop, calls=%fused_computation.144 | loop fusion | flops 18278400 | bytes 9596928 | tf_op jit(solution)/shard_map/reduce_sum | solution.py:87
  489.4 4.9 fusion.125
  494.3 5.7 fusion.134
  513.2 9.0 %collective-permute-done.15 = f32[4,3,4608]{2,1,0:T(4,128)S(1)} collective-permute-done((f32[4,3,4608]{2,1,0:T(4,128)S(1)}, f32[4,3,4608]{2,1,0:T(4,128)S(1)}, u32[]{:S(2)}, u32[]{:S(2)}) %collective-permute-start.15) | collective-permute-done | bytes 221216 | tf_op jit(solution)/shard_map/ppermute | solution.py:13
  549.5 7.4 %collective-permute-done.33 = bf16[2,2,96,768]{3,2,0,1:T(8,128)(2,1)S(1)} collective-permute-done((bf16[2,2,96,768]{3,2,0,1:T(8,128)(2,1)S(1)}, bf16[2,2,96,768]{3,2,0,1:T(8,128)(2,1)S(1)}, u32[]{:S(2)}, u32[]{:S(2)}) %collective-permute-start.33) | collective-permute-done | bytes 589856 | tf_op jit(solution)/shard_map/ppermute | solution.py:13
  566.9 5.4 collective-permute-done.35
  573.2 4.6 collective-permute-done.28
  (540 shorter events, 318.7 us)
Async XLA Ops:
  26.5 6.3 %collective-permute-start.1 = (bf16[3,1,18,768]{3,2,1,0:T(8,128)(2,1)S(1)}, bf16[3,1,18,768]{3,2,1,0:T(8,128)(2,1)S(1)}, u32[]{:S(2)}, u32[]{:S(2)}) collective-permute-start(bf16[3,1,18,768]{3,2,1,0:T(8,128)(2,1)S(1)} %fusion.121), channel_id=1, source_target_pairs={{0,2},{1,3},{2,0},{3,1},{4,6},{5,7},{6,4},{7,5},{8,10},{9,11},{10,... | collective-permute-start | bytes 248840 | tf_op jit(solution)/shard_map/ppermute | solution.py:13
  47.6 20.4 %all-to-all-start = ((bf16[3,4,64,768]{3,2,0,1:T(8,128)(2,1)}), bf16[3,4,64,768]{3,2,0,1:T(8,128)(2,1)}, u32[]{:S(2)}, u32[]{:S(2)}) async-start(bf16[3,4,64,768]{3,2,0,1:T(8,128)(2,1)} %bitcast.322), calls=%async_computation | async-start | bytes 2359296 | tf_op jit(solution)/shard_map/all_to_all | solution.py:96
  53.5 57.5 %collective-permute-start.10 = (bf16[1,3,768]{2,1,0:T(4,128)(2,1)}, bf16[1,3,768]{2,1,0:T(4,128)(2,1)}, u32[]{:S(2)}, u32[]{:S(2)}) collective-permute-start(bf16[1,3,768]{2,1,0:T(4,128)(2,1)} %fusion.163), channel_id=1, source_target_pairs={{0,4},{4,0},{8,12},{12,8},{16,20},{20,16},{24,28},{28,24},{1,5},{5... | collective-permute-start | bytes 13832 | tf_op jit(solution)/shard_map/ppermute | solution.py:13
  102.2 20.7 %all-to-all-start.1 = ((bf16[3,4,64,768]{3,2,0,1:T(8,128)(2,1)}), bf16[3,4,64,768]{3,2,0,1:T(8,128)(2,1)}, u32[]{:S(2)}, u32[]{:S(2)}) async-start(bf16[3,4,64,768]{3,2,0,1:T(8,128)(2,1)} %copy.110), calls=%async_computation.1 | async-start | bytes 2359296 | tf_op jit(solution)/shard_map/all_to_all | solution.py:103
  112.9 28.7 %collective-permute-start.11 = (bf16[2,3,768]{2,1,0:T(4,128)(2,1)}, bf16[2,3,768]{2,1,0:T(4,128)(2,1)}, u32[]{:S(2)}, u32[]{:S(2)}) collective-permute-start(bf16[2,3,768]{2,1,0:T(4,128)(2,1)} %pad_maximum_fusion.27), channel_id=1, source_target_pairs={{0,8},{4,12},{8,0},{12,4},{16,24},{20,28},{24,16},{28,20},{1,9},{5... | collective-permute-start | bytes 27656 | tf_op jit(solution)/shard_map/ppermute | solution.py:13
  148.0 12.6 %collective-permute-start.3 = (bf16[3,1,18,3072]{3,2,1,0:T(8,128)(2,1)}, bf16[3,1,18,3072]{3,2,1,0:T(8,128)(2,1)}, u32[]{:S(2)}, u32[]{:S(2)}) collective-permute-start(bf16[3,1,18,3072]{3,2,1,0:T(8,128)(2,1)} %fusion.110), channel_id=1, source_target_pairs={{0,2},{1,3},{2,0},{3,1},{4,6},{5,7},{6,4},{7,5},{8,10},{9,11},{10,... | collective-permute-start | bytes 995336 | tf_op jit(solution)/shard_map/ppermute | solution.py:13
  237.2 29.4 %collective-permute-start.5 = (bf16[3,1,18,3072]{3,2,1,0:T(8,128)(2,1)}, bf16[3,1,18,3072]{3,2,1,0:T(8,128)(2,1)}, u32[]{:S(2)}, u32[]{:S(2)}) collective-permute-start(bf16[3,1,18,3072]{3,2,1,0:T(8,128)(2,1)} %fusion.109), channel_id=1, source_target_pairs={{0,2},{1,3},{2,0},{3,1},{4,6},{5,7},{6,4},{7,5},{8,10},{9,11},{10,... | collective-permute-start | bytes 995336 | tf_op jit(solution)/shard_map/ppermute | solution.py:13
  266.4 146.1 %collective-permute-start.31 = (bf16[2,2,2,2,96,768]{5,4,0,1,2,3:T(8,128)(2,1)}, bf16[2,2,2,2,96,768]{5,4,0,1,2,3:T(8,128)(2,1)}, u32[]{:S(2)}, u32[]{:S(2)}) collective-permute-start(bf16[2,2,2,2,96,768]{5,4,0,1,2,3:T(8,128)(2,1)} %bitcast.295), channel_id=1, source_target_pairs={{0,1},{1,0},{2,3},{3,2},{4,5},{5,4},{6,7},{7,6},{8,9},{9,8},{10,11... | collective-permute-start | bytes 7077896 | tf_op jit(solution)/shard_map/ppermute | solution.py:13
  331.7 20.4 %all-to-all-start.2 = ((bf16[3,4,64,768]{3,2,0,1:T(8,128)(2,1)}), bf16[3,4,64,768]{3,2,0,1:T(8,128)(2,1)}, u32[]{:S(2)}, u32[]{:S(2)}) async-start(bf16[3,4,64,768]{3,2,0,1:T(8,128)(2,1)} %bitcast.321), calls=%async_computation.2 | async-start | bytes 2359296 | tf_op jit(solution)/shard_map/all_to_all | solution.py:96
  347.1 160.6 %collective-permute-start.26 = (bf16[2,2,2,2,24,3072]{5,4,0,1,3,2:T(8,128)(2,1)}, bf16[2,2,2,2,24,3072]{5,4,0,1,3,2:T(8,128)(2,1)}, u32[]{:S(2)}, u32[]{:S(2)}) collective-permute-start(bf16[2,2,2,2,24,3072]{5,4,0,1,3,2:T(8,128)(2,1)} %bitcast.296), channel_id=1, source_target_pairs={{0,1},{1,0},{2,3},{3,2},{4,5},{5,4},{6,7},{7,6},{8,9},{9,8},{10,11... | collective-permute-start | bytes 7077896 | tf_op jit(solution)/shard_map/ppermute | solution.py:13
  399.8 20.9 %all-to-all-start.3 = ((bf16[3,4,64,768]{3,2,0,1:T(8,128)(2,1)}), bf16[3,4,64,768]{3,2,0,1:T(8,128)(2,1)}, u32[]{:S(2)}, u32[]{:S(2)}) async-start(bf16[3,4,64,768]{3,2,0,1:T(8,128)(2,1)} %copy.127), calls=%async_computation.3 | async-start | bytes 2359296 | tf_op jit(solution)/shard_map/all_to_all | solution.py:103
  412.0 88.0 %collective-permute-start.16 = (bf16[2,2,2,2,24,1536]{5,4,3,2,1,0:T(8,128)(2,1)}, bf16[2,2,2,2,24,1536]{5,4,3,2,1,0:T(8,128)(2,1)}, u32[]{:S(2)}, u32[]{:S(2)}) collective-permute-start(bf16[2,2,2,2,24,1536]{5,4,3,2,1,0:T(8,128)(2,1)} %dynamic-slice_bitcast_fusion.2), channel_id=1, source_target_pairs={{0,1},{1,0},{2,3},{3,2},{4,5},{5,4},{6,7},{7,6},{8,9},{9,8},{10,11... | collective-permute-start | bytes 3538952 | tf_op jit(solution)/shard_map/ppermute | solution.py:13
  418.7 113.7 %collective-permute-start.32 = (bf16[2,2,2,96,768]{4,3,0,1,2:T(8,128)(2,1)}, bf16[2,2,2,96,768]{4,3,0,1,2:T(8,128)(2,1)}, u32[]{:S(2)}, u32[]{:S(2)}) collective-permute-start(bf16[2,2,2,96,768]{4,3,0,1,2:T(8,128)(2,1)} %dynamic-slice_bitcast_fusion), channel_id=1, source_target_pairs={{0,2},{1,3},{2,0},{3,1},{4,6},{5,7},{6,4},{7,5},{8,10},{9,11},{10,... | collective-permute-start | bytes 3538952 | tf_op jit(solution)/shard_map/ppermute | solution.py:13
  437.7 24.8 %collective-permute-start.6 = (bf16[3,16,1,768]{3,2,1,0:T(2,128)(2,1)}, bf16[3,16,1,768]{3,2,1,0:T(2,128)(2,1)}, u32[]{:S(2)}, u32[]{:S(2)}) collective-permute-start(bf16[3,16,1,768]{3,2,1,0:T(2,128)(2,1)} %broadcast_select_fusion.11), channel_id=1, source_target_pairs={{0,1},{1,0},{2,3},{3,2},{4,5},{5,4},{6,7},{7,6},{8,9},{9,8},{10,11... | collective-permute-start | bytes 221192 | tf_op jit(solution)/shard_map/ppermute | solution.py:13
  463.8 5.5 collective-permute-start.7
  466.5 72.2 %collective-permute-start.21 = (bf16[2,2,2,2,24,1664]{5,4,0,1,2,3:T(8,128)(2,1)}, bf16[2,2,2,2,24,1664]{5,4,0,1,2,3:T(8,128)(2,1)}, u32[]{:S(2)}, u32[]{:S(2)}) collective-permute-start(bf16[2,2,2,2,24,1664]{5,4,0,1,2,3:T(8,128)(2,1)} %bitcast.297), channel_id=1, source_target_pairs={{0,1},{1,0},{2,3},{3,2},{4,5},{5,4},{6,7},{7,6},{8,9},{9,8},{10,11... | collective-permute-start | bytes 3833864 | tf_op jit(solution)/shard_map/ppermute | solution.py:13
  487.8 13.8 %collective-permute-start.13 = (f32[1,3,4608]{2,1,0:T(4,128)S(1)}, f32[1,3,4608]{2,1,0:T(4,128)S(1)}, u32[]{:S(2)}, u32[]{:S(2)}) collective-permute-start(f32[1,3,4608]{2,1,0:T(4,128)S(1)} %bitcast.328), channel_id=1, source_target_pairs={{0,4},{4,0},{8,12},{12,8},{16,20},{20,16},{24,28},{28,24},{1,5},{5... | collective-permute-start | bytes 165896 | tf_op jit(solution)/shard_map/ppermute | solution.py:13
  501.7 5.4 collective-permute-start.14
  504.2 24.9 %collective-permute-start.17 = (bf16[2,2,2,24,1536]{4,3,2,1,0:T(8,128)(2,1)}, bf16[2,2,2,24,1536]{4,3,2,1,0:T(8,128)(2,1)}, u32[]{:S(2)}, u32[]{:S(2)}) collective-permute-start(bf16[2,2,2,24,1536]{4,3,2,1,0:T(8,128)(2,1)} %dynamic-slice_bitcast_fusion.6), channel_id=1, source_target_pairs={{0,4},{4,0},{8,12},{12,8},{16,20},{20,16},{24,28},{28,24},{1,5},{5... | collective-permute-start | bytes 1769480 | tf_op jit(solution)/shard_map/ppermute | solution.py:13
  507.3 15.0 %collective-permute-start.15 = (f32[4,3,4608]{2,1,0:T(4,128)S(1)}, f32[4,3,4608]{2,1,0:T(4,128)S(1)}, u32[]{:S(2)}, u32[]{:S(2)}) collective-permute-start(f32[4,3,4608]{2,1,0:T(4,128)S(1)} %pad_maximum_fusion.18), channel_id=1, source_target_pairs={{0,16},{4,20},{8,24},{12,28},{16,0},{20,4},{24,8},{28,12},{1,17},{... | collective-permute-start | bytes 663560 | tf_op jit(solution)/shard_map/ppermute | solution.py:13
  512.8 44.9 %collective-permute-start.27 = (bf16[2,2,2,24,3072]{4,3,0,1,2:T(8,128)(2,1)}, bf16[2,2,2,24,3072]{4,3,0,1,2:T(8,128)(2,1)}, u32[]{:S(2)}, u32[]{:S(2)}) collective-permute-start(bf16[2,2,2,24,3072]{4,3,0,1,2:T(8,128)(2,1)} %dynamic-slice_bitcast_fusion.1), channel_id=1, source_target_pairs={{0,4},{4,0},{8,12},{12,8},{16,20},{20,16},{24,28},{28,24},{1,5},{5... | collective-permute-start | bytes 3538952 | tf_op jit(solution)/shard_map/ppermute | solution.py:13
  530.6 8.0 %collective-permute-start.18 = (bf16[2,2,24,1536]{3,2,1,0:T(8,128)(2,1)S(1)}, bf16[2,2,24,1536]{3,2,1,0:T(8,128)(2,1)S(1)}, u32[]{:S(2)}, u32[]{:S(2)}) collective-permute-start(bf16[2,2,24,1536]{3,2,1,0:T(8,128)(2,1)S(1)} %dynamic-slice_bitcast_fusion.10), channel_id=1, source_target_pairs={{0,2},{1,3},{2,0},{3,1},{4,6},{5,7},{6,4},{7,5},{8,10},{9,11},{10,... | collective-permute-start | bytes 884744 | tf_op jit(solution)/shard_map/ppermute | solution.py:13
  534.0 23.0 %collective-permute-start.33 = (bf16[2,2,96,768]{3,2,0,1:T(8,128)(2,1)S(1)}, bf16[2,2,96,768]{3,2,0,1:T(8,128)(2,1)S(1)}, u32[]{:S(2)}, u32[]{:S(2)}) collective-permute-start(bf16[2,2,96,768]{3,2,0,1:T(8,128)(2,1)S(1)} %dynamic-slice_bitcast_fusion.4), channel_id=1, source_target_pairs={{0,4},{4,0},{8,12},{12,8},{16,20},{20,16},{24,28},{28,24},{1,5},{5... | collective-permute-start | bytes 1769480 | tf_op jit(solution)/shard_map/ppermute | solution.py:13
  543.9 5.6 collective-permute-start.20
  545.0 14.9 %collective-permute-start.22 = (bf16[2,2,2,24,1664]{4,3,0,1,2:T(8,128)(2,1)S(1)}, bf16[2,2,2,24,1664]{4,3,0,1,2:T(8,128)(2,1)S(1)}, u32[]{:S(2)}, u32[]{:S(2)}) collective-permute-start(bf16[2,2,2,24,1664]{4,3,0,1,2:T(8,128)(2,1)S(1)} %dynamic-slice_bitcast_fusion.3), channel_id=1, source_target_pairs={{0,2},{1,3},{2,0},{3,1},{4,6},{5,7},{6,4},{7,5},{8,10},{9,11},{10,... | collective-permute-start | bytes 1916936 | tf_op jit(solution)/shard_map/ppermute | solution.py:13
  557.1 7.5 %collective-permute-start.34 = (bf16[2,96,768]{2,1,0:T(8,128)(2,1)S(1)}, bf16[2,96,768]{2,1,0:T(8,128)(2,1)S(1)}, u32[]{:S(2)}, u32[]{:S(2)}) collective-permute-start(bf16[2,96,768]{2,1,0:T(8,128)(2,1)S(1)} %dynamic-slice_bitcast_fusion.8), channel_id=1, source_target_pairs={{0,8},{4,12},{8,0},{12,4},{16,24},{20,28},{24,16},{28,20},{1,9},{5... | collective-permute-start | bytes 884744 | tf_op jit(solution)/shard_map/ppermute | solution.py:13
  560.1 12.9 %collective-permute-start.23 = (bf16[2,2,24,1664]{3,2,0,1:T(8,128)(2,1)S(1)}, bf16[2,2,24,1664]{3,2,0,1:T(8,128)(2,1)S(1)}, u32[]{:S(2)}, u32[]{:S(2)}) collective-permute-start(bf16[2,2,24,1664]{3,2,0,1:T(8,128)(2,1)S(1)} %dynamic-slice_bitcast_fusion.7), channel_id=1, source_target_pairs={{0,4},{4,0},{8,12},{12,8},{16,20},{20,16},{24,28},{28,24},{1,5},{5... | collective-permute-start | bytes 958472 | tf_op jit(solution)/shard_map/ppermute | solution.py:13
  564.7 7.6 %collective-permute-start.35 = (bf16[96,768]{1,0:T(8,128)(2,1)S(1)}, bf16[96,768]{1,0:T(8,128)(2,1)S(1)}, u32[]{:S(2)}, u32[]{:S(2)}) collective-permute-start(bf16[96,768]{1,0:T(8,128)(2,1)S(1)} %dynamic-slice_bitcast_fusion.12), channel_id=1, source_target_pairs={{0,16},{4,20},{8,24},{12,28},{16,0},{20,4},{24,8},{28,12},{1,17},{... | collective-permute-start | bytes 442376 | tf_op jit(solution)/shard_map/ppermute | solution.py:13
  565.2 12.6 %collective-permute-start.28 = (bf16[2,2,24,3072]{3,2,0,1:T(8,128)(2,1)S(1)}, bf16[2,2,24,3072]{3,2,0,1:T(8,128)(2,1)S(1)}, u32[]{:S(2)}, u32[]{:S(2)}) collective-permute-start(bf16[2,2,24,3072]{3,2,0,1:T(8,128)(2,1)S(1)} %dynamic-slice_bitcast_fusion.5), channel_id=1, source_target_pairs={{0,2},{1,3},{2,0},{3,1},{4,6},{5,7},{6,4},{7,5},{8,10},{9,11},{10,... | collective-permute-start | bytes 1769480 | tf_op jit(solution)/shard_map/ppermute | solution.py:13
  578.6 5.7 collective-permute-start.25
  580.7 6.8 %collective-permute-start.29 = (bf16[2,24,3072]{2,1,0:T(8,128)(2,1)S(1)}, bf16[2,24,3072]{2,1,0:T(8,128)(2,1)S(1)}, u32[]{:S(2)}, u32[]{:S(2)}) collective-permute-start(bf16[2,24,3072]{2,1,0:T(8,128)(2,1)S(1)} %dynamic-slice_bitcast_fusion.9), channel_id=1, source_target_pairs={{0,8},{4,12},{8,0},{12,4},{16,24},{20,28},{24,16},{28,20},{1,9},{5... | collective-permute-start | bytes 884744 | tf_op jit(solution)/shard_map/ppermute | solution.py:13
  589.0 7.9 %collective-permute-start.30 = (bf16[24,3072]{1,0:T(8,128)(2,1)}, bf16[24,3072]{1,0:T(8,128)(2,1)}, u32[]{:S(2)}, u32[]{:S(2)}) collective-permute-start(bf16[24,3072]{1,0:T(8,128)(2,1)} %dynamic-slice_bitcast_fusion.13), channel_id=1, source_target_pairs={{0,16},{4,20},{8,24},{12,28},{16,0},{20,4},{24,8},{28,12},{1,17},{... | collective-permute-start | bytes 442376 | tf_op jit(solution)/shard_map/ppermute | solution.py:13
  (148 other events, 1106.3 us)
where the time goes:
time: 608 us; the launch traced here: 599 us
  other arithmetic  158 us (26%)
  local copies, waits for them, and re-layouts  151 us (25%)
  matrix products  145 us (24%)
  waiting for transfers between devices  91.6 us (15%)
  starting transfers between devices  49.7 us (8%)
    ppermute x36, waiting for transfers between devices, from_partner(): lax.ppermute(shard, axis, [(i, i ^ 1 << bit) for i in range(lax.axis_size...  69.2 us
    dot_general x1, matrix products, shards(): jnp.einsum('ixyd,fd->ixyf', d_branch_two, w_down, preferred_element_type=...  35.1 us
    ppermute x36, starting transfers between devices, from_partner(): lax.ppermute(shard, axis, [(i, i ^ 1 << bit) for i in range(lax.axis_size...  31.4 us
    concatenate x4, other arithmetic, extend(): return jnp.concatenate([top_rim, widened, bottom_rim], 1)  27.2 us
    unnamed x288, local copies, waits for them, and re-layouts  22.7 us
    another operation x22, local copies, waits for them, and re-layouts, tap_grads(): return jnp.stack(columns, 1)  19.4 us
    convert_element_type x1, other arithmetic, shards(): apply_taps(d_padded_ffn, conv_ffn, half_side, True).astype(jnp.bfloat16)  15.8 us
    add x1, other arithmetic, apply_taps(): summed = summed + window * weights_f[:, stencil]  15.6 us
  transfers between devices with their start and end apart: 40, of which 22 were waited for; matrix products, arithmetic and copies ran while one was open for 55% of the time, Pallas kernels for 0%

commit v1 on v0

--- a/solution.py
+++ b/solution.py
@@ -7,6 +7,28 @@
 HEADS = 12
 HEAD_DIM = 64
 epsilon = 1e-06
+
+
+def split_up(array, dim, size):
+    before, after = (array.shape[:dim], array.shape[dim + 1 :])
+    return jnp.moveaxis(array.reshape(*before, size, -1, *after), dim, 0)
+
+
+def in_order(pieces, dim):
+    pieces = jnp.moveaxis(pieces, 0, dim)
+    dims = pieces.shape
+    return pieces.reshape(*dims[:dim], dims[dim] * dims[dim + 1], *dims[dim + 2 :])
+
+
+def pairwise_exchange(value, axis, split_dim, concat_dim):
+    length, mine = (lax.axis_size(axis), lax.axis_index(axis))
+    pieces = split_up(value, split_dim, length)
+    outs = [pieces[mine]]
+    for turn in range(1, length):
+        sent = pieces[mine ^ turn]
+        outs.append(lax.ppermute(sent, axis, [(i, i ^ turn) for i in range(length)]))
+    pieces = jnp.stack(outs)[mine ^ jnp.arange(length)]
+    return in_order(pieces, concat_dim)
 
 
 def from_partner(shard, axis, bit):
@@ -93,7 +115,7 @@
     quarter = side_len // 2
     pieces = field_map.reshape(count, quarter, 2, quarter, 2, channels).transpose(0, 2, 4, 1, 3, 5)
     pieces = pieces.reshape(count, 4, quarter * quarter, channels)
-    incoming = lax.all_to_all(pieces, "narrow", split_axis=1, concat_axis=1, tiled=True)
+    incoming = pairwise_exchange(pieces, "narrow", 1, 1)
     return incoming.reshape(count, 4 * quarter * quarter, channels)
 
 

time: 608 us -> 642 us (1.056)
  waiting for transfers between devices: 91.6 us -> 127 us
    ppermute x36, waiting for transfers between devices: 69.2 us -> 94 us  [from_partner(): lax.ppermute(shard, axis, [(i, i ^ 1 << bit) for i in range(lax.axis_size...]
    ppermute x0 -> x6, waiting for transfers between devices: none -> 18.2 us  [pairwise_exchange(): lax.ppermute(sent, axis, [(i, i ^ turn) for i in range(length)])]
    all_to_all x2 -> x0, waiting for transfers between devices: 14.2 us -> none  [to_groups(): lax.all_to_all(pieces, 'narrow', split_axis=1, concat_axis=1, tiled=True)]
    all_to_all x2 -> x0, starting transfers between devices: 9.02 us -> none  [to_groups(): lax.all_to_all(pieces, 'narrow', split_axis=1, concat_axis=1, tiled=True)]
    all_to_all x2 -> x0, local copies, waits for them, and re-layouts: 6.51 us -> none  [to_groups(): lax.all_to_all(pieces, 'narrow', split_axis=1, concat_axis=1, tiled=True)]
    unnamed x288 -> x296, local copies, waits for them, and re-layouts: 22.7 us -> 19.5 us
  transfers between devices with their start and end apart: 40 -> 44, of which waited for: 22 -> 19; matrix products, arithmetic and copies ran while one was open for 55% -> 53% of each run, Pallas kernels for 0% -> 0%
where the time goes in v1:
time: 642 us; the launch traced here: 635 us
  other arithmetic  162 us (25%)
  local copies, waits for them, and re-layouts  149 us (23%)
  matrix products  146 us (23%)
  waiting for transfers between devices  127 us (20%)
  starting transfers between devices  48.1 us (7%)
    ppermute x36, waiting for transfers between devices, from_partner(): lax.ppermute(shard, axis, [(i, i ^ 1 << bit) for i in range(lax.axis_size...  94 us
    dot_general x1, matrix products, shards(): jnp.einsum('ixyd,fd->ixyf', d_branch_two, w_down, preferred_element_type=...  35.4 us
    ppermute x36, starting transfers between devices, from_partner(): lax.ppermute(shard, axis, [(i, i ^ 1 << bit) for i in range(lax.axis_size...  34.9 us
    concatenate x4, other arithmetic, extend(): return jnp.concatenate([top_rim, widened, bottom_rim], 1)  27.5 us
    unnamed x296, local copies, waits for them, and re-layouts  19.5 us
    another operation x22, local copies, waits for them, and re-layouts, tap_grads(): return jnp.stack(columns, 1)  19.4 us
    ppermute x6, waiting for transfers between devices, pairwise_exchange(): lax.ppermute(sent, axis, [(i, i ^ turn) for i in range(length)])  18.2 us
    convert_element_type x1, other arithmetic, shards(): apply_taps(d_padded_ffn, conv_ffn, half_side, True).astype(jnp.bfloat16)  16 us
  transfers between devices with their start and end apart: 44, of which 19 were waited for; matrix products, arithmetic and copies ran while one was open for 53% of the time, Pallas kernels for 0%

profile of v1, /device:TPU:0, one launch (start us, length us, event | category | flops | bytes accessed | tf_op | source)
XLA Modules:
  0.0 635.1 jit_solution(355455117903117123)
XLA Ops:
  56.2 6.6 %collective-permute-done.3 = bf16[3,1,64,768]{3,2,0,1:T(8,128)(2,1)S(1)} collective-permute-done((bf16[3,1,64,768]{3,2,0,1:T(8,128)(2,1)S(1)}, bf16[3,1,64,768]{3,2,0,1:T(8,128)(2,1)S(1)}, u32[]{:S(2)}, u32[]{:S(2)}) %collective-permute-start.3) | collective-permute-done | bytes 294944 | tf_op jit(solution)/shard_map/ppermute | solution.py:29
  73.6 5.8 copy.106
  95.9 5.1 copy.111
  113.5 8.2 %all-to-all-done = bf16[3,4,64,768]{3,2,0,1:T(8,128)(2,1)} async-done(((bf16[3,4,64,768]{3,2,0,1:T(8,128)(2,1)}), bf16[3,4,64,768]{3,2,0,1:T(8,128)(2,1)}, u32[]{:S(2)}, u32[]{:S(2)}) %all-to-all-start) | async-done | bytes 1179680 | tf_op jit(solution)/shard_map/all_to_all | solution.py:125
  128.9 5.0 fusion.143
  148.7 10.8 %collective-permute-done.6 = bf16[3,1,18,3072]{3,2,1,0:T(8,128)(2,1)} collective-permute-done((bf16[3,1,18,3072]{3,2,1,0:T(8,128)(2,1)}, bf16[3,1,18,3072]{3,2,1,0:T(8,128)(2,1)}, u32[]{:S(2)}, u32[]{:S(2)}) %collective-permute-start.6) | collective-permute-done | bytes 331808 | tf_op jit(solution)/shard_map/ppermute | solution.py:35
  160.6 12.1 %maximum_maximum_fusion = (bf16[3,17,18,3072]{3,2,1,0:T(8,128)(2,1)S(1)}, bf16[3,17,18,3072]{3,2,1,0:T(8,128)(2,1)S(1)}) fusion(bf16[3,16,1,3072]{3,2,1,0:T(2,128)(2,1)} %copy-done.25, bf16[3,16,16,3072]{3,2,1,0:T(8,128)(2,1)} %copy-done.5, bf16[3,16,1,3072]{3,2,1,0:T(2,128)(2,1)} %copy-done.23, bf16[3,1,18,3072]{3,2,1,0:T(8,128)(2,1)S(1)} %get-tuple-element.129, ...), kind=kLoop, calls=%fused_computation.63 | loop fusion | flops 45121536 | bytes 17252352 | tf_op jit(solution)/shard_map/concatenate | solution.py:81
  172.9 15.6 %fusion.7 = f32[3,16,16,3072]{3,2,1,0:T(8,128)} fusion(bf16[3,16,16,3072]{3,2,1,0:T(8,128)(2,1)S(1)} %bitcast.342, bf16[3,16,1,3072]{3,2,1,0:T(2,128)(2,1)} %copy-done.25, bf16[3,16,1,3072]{3,2,1,0:T(2,128)(2,1)S(1)} %copy-done.24, f32[3072]{0:T(1024)S(1)} %bitcast.396, f32[3072]{0:T(1024)S(1)} %bitcast.394, f32[3072]{0:T(1024)S(1)} %bitcast.392, ...), kind=kLoop, calls=%fused_computation.30 | loop fusion | flops 75497472 | bytes 43167744 | tf_op jit(solution)/shard_map/add | solution.py:96
  188.5 35.4 %fusion.29 = (bf16[3072]{0:T(1024)(128)(2,1)}, bf16[3072]{0:T(1024)(128)(2,1)}, bf16[3072]{0:T(1024)(128)(2,1)}, bf16[3072]{0:T(1024)(128)(2,1)}, bf16[3072]{0:T...) fusion(bf16[3,17,18,3072]{3,2,1,0:T(8,128)(2,1)} %copy-done.4, ...), kind=kOutput, calls=%fused_computation.52 | convolution fusion | flops 3753612288 | bytes 53738508 | tf_op jit(solution)/shard_map/ixyd,fd->ixyf/dot_general | solution.py:247
  236.8 9.7 %bitcast_convert_fusion = bf16[3072,768]{1,0:T(8,128)(2,1)} fusion(bf16[3,16,16,768]{3,2,1,0:T(8,128)(2,1)S(1)} %bitcast.401, f32[3]{0:T(128)S(1)} %compare_convert_fusion, f32[3,768]{1,0:T(4,128)S(1)} %copy-done.115, f32[3,16,16,3072]{3,2,1,0:T(8,128)} %fusion.7), kind=kOutput, calls=%fused_computation.53 | convolution fusion | flops 3649830912 | bytes 15344652 | tf_op jit(solution)/shard_map/ixyf,ixyd->fd/dot_general | solution.py:244
  267.0 10.0 %pad_maximum_fusion.1 = (bf16[3,17,18,3072]{3,2,1,0:T(8,128)(2,1)S(1)}, bf16[3,17,18,3072]{3,2,1,0:T(8,128)(2,1)S(1)}) fusion(bf16[3,1,18,3072]{3,2,1,0:T(8,128)(2,1)S(1)} %get-tuple-element.127, bf16[3,16,1,3072]{3,2,1,0:T(2,128)(2,1)S(1)} %copy-done.29, bf16[3,16,16,3072]{3,2,1,0:T(8,128)(2,1)S(1)} %bitcast.340, ...), kind=kLoop, calls=%fused_computation.65 | loop fusion | flops 45121536 | bytes 17252352 | tf_op jit(solution)/shard_map/concatenate | solution.py:81
  277.1 16.0 %fusion.20 = bf16[3,16,16,3072]{3,2,1,0:T(8,128)(2,1)} fusion(bf16[3,16,16,3072]{3,2,1,0:T(8,128)(2,1)S(1)} %bitcast.340, bf16[3,17,18,3072]{3,2,1,0:T(8,128)(2,1)S(1)} %get-tuple-element.100, bf16[3,16,1,3072]{3,2,1,0:T(2,128)(2,1)S(1)} %copy-done.27, bf16[3,16,1,3072]{3,2,1,0:T(2,128)(2,1)} %copy-done.28, ...), kind=kLoop, calls=%fused_computation.43 | loop fusion | flops 77856768 | bytes 38449152 | tf_op jit(solution)/shard_map/convert_element_type | solution.py:257
  293.2 8.6 %multiply_reduce_fusion.5 = (f32[3,16,16]{2,1,0:T(8,128)S(1)}, f32[3,16,16,768]{3,2,1,0:T(8,128)S(1)}) fusion(f32[3,16,16,768]{3,2,1,0:T(8,128)} %copy-done.12, f32[3,768]{1,0:T(4,128)S(1)} %copy-done.95, f32[3,16,16]{2,1,0:T(8,128)S(1)} %copy-done.54, bf16[3,16,16,3072]{3,2,1,0:T(8,128)(2,1)} %fusion.20, bf16[768,3072]{1,0:T(8,128)(2,1)} %param.17), kind=kOutput, calls=%fused_computation.172 | convolution fusion | flops 3626237184 | bytes 14171136 | tf_op jit(solution)/shard_map/ixyf,df->ixyd/dot_general | solution.py:259
  303.9 11.7 %fusion.86 = (f32[3,768]{1,0:T(4,128)}, bf16[3,16,16,768]{3,2,1,0:T(8,128)(2,1)}, f32[3,768]{1,0:T(4,128)}, f32[3,16,16,768]{3,2,1,0:T(8,128)S(1)}) fusion(bf16[3,16,16,768]{3,2,1,0:T(8,128)(2,1)S(1)} %bitcast.402, f32[3]{0:T(128)S(1)} %compare_convert_fusion, f32[3,16,16,768]{3,2,1,0:T(8,128)S(1)} %copy-done.13, f32[3,768]{1,0:T(4,128)S(1)} %copy-done.116, ...), kind=kOutput, calls=%fused_computation.161 | convolution fusion | flops 3655724544 | bytes 26001420 | tf_op jit(solution)/shard_map/dot_general | solution.py:237
  319.9 6.4 %bitcast_convert_fusion.1 = bf16[768,3072]{1,0:T(8,128)(2,1)} fusion(bf16[3,16,16,3072]{3,2,1,0:T(8,128)(2,1)S(1)} %bitcast.351, f32[3,16,16,768]{3,2,1,0:T(8,128)S(1)} %copy-done.13, f32[3,768]{1,0:T(4,128)S(1)} %copy-done.118, f32[3,768]{1,0:T(4,128)S(1)} %copy-done.95, f32[3,16,16]{2,1,0:T(8,128)S(1)} %copy-done.82, f32[3,16,16]{2,1,0:T(8,128)S(1)} %copy-done.54), kind=kOutput, calls=%fused_computation.54 | convolution fusion | flops 3629187072 | bytes 11821056 | tf_op jit(solution)/shard_map/ixyd,ixyf->df/dot_general | solution.py:258
  340.8 6.7 %collective-permute-done.10 = bf16[3,1,64,768]{3,2,0,1:T(8,128)(2,1)S(1)} collective-permute-done((bf16[3,1,64,768]{3,2,0,1:T(8,128)(2,1)S(1)}, bf16[3,1,64,768]{3,2,0,1:T(8,128)(2,1)S(1)}, u32[]{:S(2)}, u32[]{:S(2)}) %collective-permute-start.10) | collective-permute-done | bytes 294944 | tf_op jit(solution)/shard_map/ppermute | solution.py:29
  351.7 5.1 copy.121
  361.4 6.8 %fusion.87 = bf16[3,256,1,12,64]{1,4,3,0,2:T(8,128)(2,1)} fusion(bf16[3,256,12,64]{1,3,2,0:T(8,128)(2,1)} %reshape_reshape_reshape.3, f32[3,12,256,256]{2,3,1,0:T(8,128)} %copy-done.1, f32[3,12,256]{2,1,0:T(8,128)} %log_add_fusion), kind=kOutput, calls=%fused_computation.184 | convolution fusion | flops 309067776 | bytes 11833344 | tf_op jit(solution)/shard_map/ihqk,iqhe->ikhe/dot_general | solution.py:274
  368.2 8.3 %multiply_reduce_fusion = (f32[3,12,256]{2,1,0:T(8,128)}, f32[3,12,256,256]{2,3,1,0:T(8,128)}) fusion(f32[3,12,256,256]{2,3,1,0:T(8,128)} %copy-done.1, f32[3,12,256]{2,1,0:T(8,128)S(1)} %copy-done.46, bf16[3,256,12,64]{1,3,2,0:T(8,128)(2,1)S(1)} %copy-done.15, bf16[3,256,3,12,64]{1,4,3,2,0:T(8,128)(2,1)} %bitcast.345), kind=kOutput, calls=%fused_computation.56 | convolution fusion | flops 311417856 | bytes 21307392 | tf_op jit(solution)/shard_map/iqhe,ikhe->ihqk/dot_general | solution.py:273
  376.5 11.3 %multiply_convert_fusion = bf16[3,12,256,256]{2,3,1,0:T(8,128)(2,1)} fusion(f32[3,12,256,256]{2,3,1,0:T(8,128)} %get-tuple-element.178, f32[3,12,256,256]{2,3,1,0:T(8,128)} %copy-done.1, f32[3,12,256]{2,1,0:T(8,128)} %get-tuple-element.177, f32[3,12,256]{2,1,0:T(8,128)} %log_add_fusion), kind=kLoop, calls=%fused_computation.55 | loop fusion | flops 11796480 | bytes 23666688 | tf_op jit(solution)/shard_map/convert_element_type | solution.py:277
  404.0 5.3 bitcast_convert_fusion.2
  413.6 6.3 all-to-all-done.1
  429.3 7.6 %fusion.78 = (bf16[768]{0:T(1024)(128)(2,1)}, bf16[768]{0:T(1024)(128)(2,1)}, bf16[768]{0:T(1024)(128)(2,1)}, bf16[768]{0:T(1024)(128)(2,1)S(1)}, bf16[768]{0:T(...) fusion(bf16[3,16,16,768]{3,2,1,0:T(8,128)(2,1)} %reshape.337, ...), kind=kLoop, calls=%fused_computation.146 | loop fusion | flops 18278400 | bytes 9596928 | tf_op jit(solution)/shard_map/reduce_sum | solution.py:109
  488.5 4.9 fusion.125
  493.4 5.7 fusion.134
  513.3 8.0 %collective-permute-done.21 = f32[4,3,4608]{2,1,0:T(4,128)S(1)} collective-permute-done((f32[4,3,4608]{2,1,0:T(4,128)S(1)}, f32[4,3,4608]{2,1,0:T(4,128)S(1)}, u32[]{:S(2)}, u32[]{:S(2)}) %collective-permute-start.21) | collective-permute-done | bytes 221216 | tf_op jit(solution)/shard_map/ppermute | solution.py:35
  530.5 14.1 %collective-permute-done.24 = bf16[2,2,24,1536]{3,2,1,0:T(8,128)(2,1)S(1)} collective-permute-done((bf16[2,2,24,1536]{3,2,1,0:T(8,128)(2,1)S(1)}, bf16[2,2,24,1536]{3,2,1,0:T(8,128)(2,1)S(1)}, u32[]{:S(2)}, u32[]{:S(2)}) %collective-permute-start.24) | collective-permute-done | bytes 294944 | tf_op jit(solution)/shard_map/ppermute | solution.py:35
  559.1 5.2 collective-permute-done.28
  568.3 22.6 %collective-permute-done.29 = bf16[2,2,24,1664]{3,2,0,1:T(8,128)(2,1)S(1)} collective-permute-done((bf16[2,2,24,1664]{3,2,0,1:T(8,128)(2,1)S(1)}, bf16[2,2,24,1664]{3,2,0,1:T(8,128)(2,1)S(1)}, u32[]{:S(2)}, u32[]{:S(2)}) %collective-permute-start.29) | collective-permute-done | bytes 319520 | tf_op jit(solution)/shard_map/ppermute | solution.py:35
  591.5 7.8 %collective-permute-done.39 = bf16[2,2,96,768]{3,2,0,1:T(8,128)(2,1)S(1)} collective-permute-done((bf16[2,2,96,768]{3,2,0,1:T(8,128)(2,1)S(1)}, bf16[2,2,96,768]{3,2,0,1:T(8,128)(2,1)S(1)}, u32[]{:S(2)}, u32[]{:S(2)}) %collective-permute-start.39) | collective-permute-done | bytes 589856 | tf_op jit(solution)/shard_map/ppermute | solution.py:35
  620.4 6.0 collective-permute-done.35
  628.3 5.9 collective-permute-done.36
  (564 shorter events, 326.7 us)
Async XLA Ops:
  47.1 9.1 %collective-permute-start.4 = (bf16[3,1,64,768]{3,2,0,1:T(8,128)(2,1)S(1)}, bf16[3,1,64,768]{3,2,0,1:T(8,128)(2,1)S(1)}, u32[]{:S(2)}, u32[]{:S(2)}) collective-permute-start(bf16[3,1,64,768]{3,2,0,1:T(8,128)(2,1)S(1)} %get-tuple-element.122), channel_id=1, source_target_pairs={{0,3},{1,2},{2,1},{3,0},{4,7},{5,6},{6,5},{7,4},{8,11},{9,10},{10,... | collective-permute-start | bytes 884744 | tf_op jit(solution)/shard_map/ppermute | solution.py:29
  47.8 14.9 %collective-permute-start.3 = (bf16[3,1,64,768]{3,2,0,1:T(8,128)(2,1)S(1)}, bf16[3,1,64,768]{3,2,0,1:T(8,128)(2,1)S(1)}, u32[]{:S(2)}, u32[]{:S(2)}) collective-permute-start(bf16[3,1,64,768]{3,2,0,1:T(8,128)(2,1)S(1)} %get-tuple-element.123), channel_id=1, source_target_pairs={{0,2},{1,3},{2,0},{3,1},{4,6},{5,7},{6,4},{7,5},{8,10},{9,11},{10,... | collective-permute-start | bytes 884744 | tf_op jit(solution)/shard_map/ppermute | solution.py:29
  49.0 13.8 %collective-permute-start.2 = (bf16[3,1,64,768]{3,2,0,1:T(8,128)(2,1)S(1)}, bf16[3,1,64,768]{3,2,0,1:T(8,128)(2,1)S(1)}, u32[]{:S(2)}, u32[]{:S(2)}) collective-permute-start(bf16[3,1,64,768]{3,2,0,1:T(8,128)(2,1)S(1)} %get-tuple-element.124), channel_id=1, source_target_pairs={{0,1},{1,0},{2,3},{3,2},{4,5},{5,4},{6,7},{7,6},{8,9},{9,8},{10,11... | collective-permute-start | bytes 884744 | tf_op jit(solution)/shard_map/ppermute | solution.py:29
  49.6 60.1 %collective-permute-start.16 = (bf16[1,3,768]{2,1,0:T(4,128)(2,1)}, bf16[1,3,768]{2,1,0:T(4,128)(2,1)}, u32[]{:S(2)}, u32[]{:S(2)}) collective-permute-start(bf16[1,3,768]{2,1,0:T(4,128)(2,1)} %fusion.164), channel_id=1, source_target_pairs={{0,4},{4,0},{8,12},{12,8},{16,20},{20,16},{24,28},{28,24},{1,5},{5... | collective-permute-start | bytes 13832 | tf_op jit(solution)/shard_map/ppermute | solution.py:35
  101.0 20.7 %all-to-all-start = ((bf16[3,4,64,768]{3,2,0,1:T(8,128)(2,1)}), bf16[3,4,64,768]{3,2,0,1:T(8,128)(2,1)}, u32[]{:S(2)}, u32[]{:S(2)}) async-start(bf16[3,4,64,768]{3,2,0,1:T(8,128)(2,1)} %copy.111), calls=%async_computation | async-start | bytes 2359296 | tf_op jit(solution)/shard_map/all_to_all | solution.py:125
  111.7 28.7 %collective-permute-start.17 = (bf16[2,3,768]{2,1,0:T(4,128)(2,1)}, bf16[2,3,768]{2,1,0:T(4,128)(2,1)}, u32[]{:S(2)}, u32[]{:S(2)}) collective-permute-start(bf16[2,3,768]{2,1,0:T(4,128)(2,1)} %pad_maximum_fusion.27), channel_id=1, source_target_pairs={{0,8},{4,12},{8,0},{12,4},{16,24},{20,28},{24,16},{28,20},{1,9},{5... | collective-permute-start | bytes 27656 | tf_op jit(solution)/shard_map/ppermute | solution.py:35
  146.8 12.6 %collective-permute-start.6 = (bf16[3,1,18,3072]{3,2,1,0:T(8,128)(2,1)}, bf16[3,1,18,3072]{3,2,1,0:T(8,128)(2,1)}, u32[]{:S(2)}, u32[]{:S(2)}) collective-permute-start(bf16[3,1,18,3072]{3,2,1,0:T(8,128)(2,1)} %fusion.110), channel_id=1, source_target_pairs={{0,2},{1,3},{2,0},{3,1},{4,6},{5,7},{6,4},{7,5},{8,10},{9,11},{10,... | collective-permute-start | bytes 995336 | tf_op jit(solution)/shard_map/ppermute | solution.py:35
  236.3 29.5 %collective-permute-start.8 = (bf16[3,1,18,3072]{3,2,1,0:T(8,128)(2,1)}, bf16[3,1,18,3072]{3,2,1,0:T(8,128)(2,1)}, u32[]{:S(2)}, u32[]{:S(2)}) collective-permute-start(bf16[3,1,18,3072]{3,2,1,0:T(8,128)(2,1)} %fusion.109), channel_id=1, source_target_pairs={{0,2},{1,3},{2,0},{3,1},{4,6},{5,7},{6,4},{7,5},{8,10},{9,11},{10,... | collective-permute-start | bytes 995336 | tf_op jit(solution)/shard_map/ppermute | solution.py:35
  265.6 241.2 %collective-permute-start.37 = (bf16[2,2,2,2,96,768]{5,4,0,1,2,3:T(8,128)(2,1)}, bf16[2,2,2,2,96,768]{5,4,0,1,2,3:T(8,128)(2,1)}, u32[]{:S(2)}, u32[]{:S(2)}) collective-permute-start(bf16[2,2,2,2,96,768]{5,4,0,1,2,3:T(8,128)(2,1)} %bitcast.330), channel_id=1, source_target_pairs={{0,1},{1,0},{2,3},{3,2},{4,5},{5,4},{6,7},{7,6},{8,9},{9,8},{10,11... | collective-permute-start | bytes 7077896 | tf_op jit(solution)/shard_map/ppermute | solution.py:35
  331.8 9.0 %collective-permute-start.11 = (bf16[3,1,64,768]{3,2,0,1:T(8,128)(2,1)S(1)}, bf16[3,1,64,768]{3,2,0,1:T(8,128)(2,1)S(1)}, u32[]{:S(2)}, u32[]{:S(2)}) collective-permute-start(bf16[3,1,64,768]{3,2,0,1:T(8,128)(2,1)S(1)} %get-tuple-element.118), channel_id=1, source_target_pairs={{0,3},{1,2},{2,1},{3,0},{4,7},{5,6},{6,5},{7,4},{8,11},{9,10},{10,... | collective-permute-start | bytes 884744 | tf_op jit(solution)/shard_map/ppermute | solution.py:29
  333.4 14.1 %collective-permute-start.10 = (bf16[3,1,64,768]{3,2,0,1:T(8,128)(2,1)S(1)}, bf16[3,1,64,768]{3,2,0,1:T(8,128)(2,1)S(1)}, u32[]{:S(2)}, u32[]{:S(2)}) collective-permute-start(bf16[3,1,64,768]{3,2,0,1:T(8,128)(2,1)S(1)} %get-tuple-element.119), channel_id=1, source_target_pairs={{0,2},{1,3},{2,0},{3,1},{4,6},{5,7},{6,4},{7,5},{8,10},{9,11},{10,... | collective-permute-start | bytes 884744 | tf_op jit(solution)/shard_map/ppermute | solution.py:29
  333.8 13.7 %collective-permute-start.9 = (bf16[3,1,64,768]{3,2,0,1:T(8,128)(2,1)S(1)}, bf16[3,1,64,768]{3,2,0,1:T(8,128)(2,1)S(1)}, u32[]{:S(2)}, u32[]{:S(2)}) collective-permute-start(bf16[3,1,64,768]{3,2,0,1:T(8,128)(2,1)S(1)} %get-tuple-element.120), channel_id=1, source_target_pairs={{0,1},{1,0},{2,3},{3,2},{4,5},{5,4},{6,7},{7,6},{8,9},{9,8},{10,11... | collective-permute-start | bytes 884744 | tf_op jit(solution)/shard_map/ppermute | solution.py:29
  340.2 206.1 %collective-permute-start.32 = (bf16[2,2,2,2,24,3072]{5,4,0,1,3,2:T(8,128)(2,1)}, bf16[2,2,2,2,24,3072]{5,4,0,1,3,2:T(8,128)(2,1)}, u32[]{:S(2)}, u32[]{:S(2)}) collective-permute-start(bf16[2,2,2,2,24,3072]{5,4,0,1,3,2:T(8,128)(2,1)} %bitcast.331), channel_id=1, source_target_pairs={{0,1},{1,0},{2,3},{3,2},{4,5},{5,4},{6,7},{7,6},{8,9},{9,8},{10,11... | collective-permute-start | bytes 7077896 | tf_op jit(solution)/shard_map/ppermute | solution.py:35
  399.5 20.4 %all-to-all-start.1 = ((bf16[3,4,64,768]{3,2,0,1:T(8,128)(2,1)}), bf16[3,4,64,768]{3,2,0,1:T(8,128)(2,1)}, u32[]{:S(2)}, u32[]{:S(2)}) async-start(bf16[3,4,64,768]{3,2,0,1:T(8,128)(2,1)} %copy.127), calls=%async_computation.1 | async-start | bytes 2359296 | tf_op jit(solution)/shard_map/all_to_all | solution.py:125
  413.1 86.0 %collective-permute-start.22 = (bf16[2,2,2,2,24,1536]{5,4,3,2,1,0:T(8,128)(2,1)}, bf16[2,2,2,2,24,1536]{5,4,3,2,1,0:T(8,128)(2,1)}, u32[]{:S(2)}, u32[]{:S(2)}) collective-permute-start(bf16[2,2,2,2,24,1536]{5,4,3,2,1,0:T(8,128)(2,1)} %dynamic-slice_bitcast_fusion.2), channel_id=1, source_target_pairs={{0,1},{1,0},{2,3},{3,2},{4,5},{5,4},{6,7},{7,6},{8,9},{9,8},{10,11... | collective-permute-start | bytes 3538952 | tf_op jit(solution)/shard_map/ppermute | solution.py:35
  436.8 24.8 %collective-permute-start.12 = (bf16[3,16,1,768]{3,2,1,0:T(2,128)(2,1)}, bf16[3,16,1,768]{3,2,1,0:T(2,128)(2,1)}, u32[]{:S(2)}, u32[]{:S(2)}) collective-permute-start(bf16[3,16,1,768]{3,2,1,0:T(2,128)(2,1)} %broadcast_select_fusion.11), channel_id=1, source_target_pairs={{0,1},{1,0},{2,3},{3,2},{4,5},{5,4},{6,7},{7,6},{8,9},{9,8},{10,11... | collective-permute-start | bytes 221192 | tf_op jit(solution)/shard_map/ppermute | solution.py:35
  465.6 83.3 %collective-permute-start.27 = (bf16[2,2,2,2,24,1664]{5,4,0,1,2,3:T(8,128)(2,1)}, bf16[2,2,2,2,24,1664]{5,4,0,1,2,3:T(8,128)(2,1)}, u32[]{:S(2)}, u32[]{:S(2)}) collective-permute-start(bf16[2,2,2,2,24,1664]{5,4,0,1,2,3:T(8,128)(2,1)} %bitcast.332), channel_id=1, source_target_pairs={{0,1},{1,0},{2,3},{3,2},{4,5},{5,4},{6,7},{7,6},{8,9},{9,8},{10,11... | collective-permute-start | bytes 3833864 | tf_op jit(solution)/shard_map/ppermute | solution.py:35
  486.9 13.8 %collective-permute-start.19 = (f32[1,3,4608]{2,1,0:T(4,128)S(1)}, f32[1,3,4608]{2,1,0:T(4,128)S(1)}, u32[]{:S(2)}, u32[]{:S(2)}) collective-permute-start(f32[1,3,4608]{2,1,0:T(4,128)S(1)} %bitcast.364), channel_id=1, source_target_pairs={{0,4},{4,0},{8,12},{12,8},{16,20},{20,16},{24,28},{28,24},{1,5},{5... | collective-permute-start | bytes 165896 | tf_op jit(solution)/shard_map/ppermute | solution.py:35
  503.4 21.1 %collective-permute-start.23 = (bf16[2,2,2,24,1536]{4,3,2,1,0:T(8,128)(2,1)}, bf16[2,2,2,24,1536]{4,3,2,1,0:T(8,128)(2,1)}, u32[]{:S(2)}, u32[]{:S(2)}) collective-permute-start(bf16[2,2,2,24,1536]{4,3,2,1,0:T(8,128)(2,1)} %dynamic-slice_bitcast_fusion.6), channel_id=1, source_target_pairs={{0,4},{4,0},{8,12},{12,8},{16,20},{20,16},{24,28},{28,24},{1,5},{5... | collective-permute-start | bytes 1769480 | tf_op jit(solution)/shard_map/ppermute | solution.py:35
  506.4 14.9 %collective-permute-start.21 = (f32[4,3,4608]{2,1,0:T(4,128)S(1)}, f32[4,3,4608]{2,1,0:T(4,128)S(1)}, u32[]{:S(2)}, u32[]{:S(2)}) collective-permute-start(f32[4,3,4608]{2,1,0:T(4,128)S(1)} %pad_maximum_fusion.18), channel_id=1, source_target_pairs={{0,16},{4,20},{8,24},{12,28},{16,0},{20,4},{24,8},{28,12},{1,17},{... | collective-permute-start | bytes 663560 | tf_op jit(solution)/shard_map/ppermute | solution.py:35
  511.7 53.4 %collective-permute-start.38 = (bf16[2,2,2,96,768]{4,3,0,1,2:T(8,128)(2,1)}, bf16[2,2,2,96,768]{4,3,0,1,2:T(8,128)(2,1)}, u32[]{:S(2)}, u32[]{:S(2)}) collective-permute-start(bf16[2,2,2,96,768]{4,3,0,1,2:T(8,128)(2,1)} %dynamic-slice_bitcast_fusion), channel_id=1, source_target_pairs={{0,2},{1,3},{2,0},{3,1},{4,6},{5,7},{6,4},{7,5},{8,10},{9,11},{10,... | collective-permute-start | bytes 3538952 | tf_op jit(solution)/shard_map/ppermute | solution.py:35
  525.9 18.6 %collective-permute-start.24 = (bf16[2,2,24,1536]{3,2,1,0:T(8,128)(2,1)S(1)}, bf16[2,2,24,1536]{3,2,1,0:T(8,128)(2,1)S(1)}, u32[]{:S(2)}, u32[]{:S(2)}) collective-permute-start(bf16[2,2,24,1536]{3,2,1,0:T(8,128)(2,1)S(1)} %dynamic-slice_bitcast_fusion.10), channel_id=1, source_target_pairs={{0,2},{1,3},{2,0},{3,1},{4,6},{5,7},{6,4},{7,5},{8,10},{9,11},{10,... | collective-permute-start | bytes 884744 | tf_op jit(solution)/shard_map/ppermute | solution.py:35
  544.6 7.7 %collective-permute-start.25 = (bf16[2,24,1536]{2,1,0:T(8,128)(2,1)S(1)}, bf16[2,24,1536]{2,1,0:T(8,128)(2,1)S(1)}, u32[]{:S(2)}, u32[]{:S(2)}) collective-permute-start(bf16[2,24,1536]{2,1,0:T(8,128)(2,1)S(1)} %dynamic-slice_bitcast_fusion.22), channel_id=1, source_target_pairs={{0,8},{4,12},{8,0},{12,4},{16,24},{20,28},{24,16},{28,20},{1,9},{5... | collective-permute-start | bytes 442376 | tf_op jit(solution)/shard_map/ppermute | solution.py:35
  550.6 13.7 %collective-permute-start.28 = (bf16[2,2,2,24,1664]{4,3,0,1,2:T(8,128)(2,1)S(1)}, bf16[2,2,2,24,1664]{4,3,0,1,2:T(8,128)(2,1)S(1)}, u32[]{:S(2)}, u32[]{:S(2)}) collective-permute-start(bf16[2,2,2,24,1664]{4,3,0,1,2:T(8,128)(2,1)S(1)} %dynamic-slice_bitcast_fusion.3), channel_id=1, source_target_pairs={{0,2},{1,3},{2,0},{3,1},{4,6},{5,7},{6,4},{7,5},{8,10},{9,11},{10,... | collective-permute-start | bytes 1916936 | tf_op jit(solution)/shard_map/ppermute | solution.py:35
  555.1 45.6 %collective-permute-start.33 = (bf16[2,2,2,24,3072]{4,3,0,1,2:T(8,128)(2,1)S(1)}, bf16[2,2,2,24,3072]{4,3,0,1,2:T(8,128)(2,1)S(1)}, u32[]{:S(2)}, u32[]{:S(2)}) collective-permute-start(bf16[2,2,2,24,3072]{4,3,0,1,2:T(8,128)(2,1)S(1)} %dynamic-slice_bitcast_fusion.1), channel_id=1, source_target_pairs={{0,4},{4,0},{8,12},{12,8},{16,20},{20,16},{24,28},{28,24},{1,5},{5... | collective-permute-start | bytes 3538952 | tf_op jit(solution)/shard_map/ppermute | solution.py:35
  564.5 26.4 %collective-permute-start.29 = (bf16[2,2,24,1664]{3,2,0,1:T(8,128)(2,1)S(1)}, bf16[2,2,24,1664]{3,2,0,1:T(8,128)(2,1)S(1)}, u32[]{:S(2)}, u32[]{:S(2)}) collective-permute-start(bf16[2,2,24,1664]{3,2,0,1:T(8,128)(2,1)S(1)} %dynamic-slice_bitcast_fusion.7), channel_id=1, source_target_pairs={{0,4},{4,0},{8,12},{12,8},{16,20},{20,16},{24,28},{28,24},{1,5},{5... | collective-permute-start | bytes 958472 | tf_op jit(solution)/shard_map/ppermute | solution.py:35
  566.8 32.6 %collective-permute-start.39 = (bf16[2,2,96,768]{3,2,0,1:T(8,128)(2,1)S(1)}, bf16[2,2,96,768]{3,2,0,1:T(8,128)(2,1)S(1)}, u32[]{:S(2)}, u32[]{:S(2)}) collective-permute-start(bf16[2,2,96,768]{3,2,0,1:T(8,128)(2,1)S(1)} %dynamic-slice_bitcast_fusion.4), channel_id=1, source_target_pairs={{0,4},{4,0},{8,12},{12,8},{16,20},{20,16},{24,28},{28,24},{1,5},{5... | collective-permute-start | bytes 1769480 | tf_op jit(solution)/shard_map/ppermute | solution.py:35
  591.0 10.2 %collective-permute-start.30 = (bf16[2,24,1664]{2,1,0:T(8,128)(2,1)S(1)}, bf16[2,24,1664]{2,1,0:T(8,128)(2,1)S(1)}, u32[]{:S(2)}, u32[]{:S(2)}) collective-permute-start(bf16[2,24,1664]{2,1,0:T(8,128)(2,1)S(1)} %dynamic-slice_bitcast_fusion.19), channel_id=1, source_target_pairs={{0,8},{4,12},{8,0},{12,4},{16,24},{20,28},{24,16},{28,20},{1,9},{5... | collective-permute-start | bytes 479240 | tf_op jit(solution)/shard_map/ppermute | solution.py:35
  600.3 17.9 %collective-permute-start.40 = (bf16[2,96,768]{2,1,0:T(8,128)(2,1)}, bf16[2,96,768]{2,1,0:T(8,128)(2,1)}, u32[]{:S(2)}, u32[]{:S(2)}) collective-permute-start(bf16[2,96,768]{2,1,0:T(8,128)(2,1)} %dynamic-slice_bitcast_fusion.8), channel_id=1, source_target_pairs={{0,8},{4,12},{8,0},{12,4},{16,24},{20,28},{24,16},{28,20},{1,9},{5... | collective-permute-start | bytes 884744 | tf_op jit(solution)/shard_map/ppermute | solution.py:35
  603.1 12.0 %collective-permute-start.34 = (bf16[2,2,24,3072]{3,2,0,1:T(8,128)(2,1)}, bf16[2,2,24,3072]{3,2,0,1:T(8,128)(2,1)}, u32[]{:S(2)}, u32[]{:S(2)}) collective-permute-start(bf16[2,2,24,3072]{3,2,0,1:T(8,128)(2,1)} %dynamic-slice_bitcast_fusion.5), channel_id=1, source_target_pairs={{0,2},{1,3},{2,0},{3,1},{4,6},{5,7},{6,4},{7,5},{8,10},{9,11},{10,... | collective-permute-start | bytes 1769480 | tf_op jit(solution)/shard_map/ppermute | solution.py:35
  616.5 9.9 %collective-permute-start.35 = (bf16[2,24,3072]{2,1,0:T(8,128)(2,1)S(1)}, bf16[2,24,3072]{2,1,0:T(8,128)(2,1)S(1)}, u32[]{:S(2)}, u32[]{:S(2)}) collective-permute-start(bf16[2,24,3072]{2,1,0:T(8,128)(2,1)S(1)} %dynamic-slice_bitcast_fusion.9), channel_id=1, source_target_pairs={{0,8},{4,12},{8,0},{12,4},{16,24},{20,28},{24,16},{28,20},{1,9},{5... | collective-permute-start | bytes 884744 | tf_op jit(solution)/shard_map/ppermute | solution.py:35
  619.3 8.2 %collective-permute-start.41 = (bf16[96,768]{1,0:T(8,128)(2,1)S(1)}, bf16[96,768]{1,0:T(8,128)(2,1)S(1)}, u32[]{:S(2)}, u32[]{:S(2)}) collective-permute-start(bf16[96,768]{1,0:T(8,128)(2,1)S(1)} %dynamic-slice_bitcast_fusion.20), channel_id=1, source_target_pairs={{0,16},{4,20},{8,24},{12,28},{16,0},{20,4},{24,8},{28,12},{1,17},{... | collective-permute-start | bytes 442376 | tf_op jit(solution)/shard_map/ppermute | solution.py:35
  (156 other events, 1117.0 us)
